TPU v7x, 128 devices: a whole 4x4x4 slice. The times are simulated.
128 devices in a mesh: ctx: 16 (over x, y), head: 8 (over z, core).
Axes of the slice: x: 4, y: 4, z: 4, core: 2. Of those that a mesh axis runs over, the one named last changes fastest.
Arguments:
- query_low: bfloat16 [2, 1536], P(None, 'ctx'), may hold values from -6 to 6
- query_weight: bfloat16 [1536, 73728], P('ctx', 'head'), may hold values from -0.21875 to 0.21875
- latent_cache: bfloat16 [2, 131072, 576], P(None, ('ctx', 'head')), may hold values from -300 to 300
- lengths: int32 [2], replicated, may hold values from 81921 to 131072
- value_weight: bfloat16 [128, 512, 128], P('head'), may hold values from -2 to 2
- output_weight: bfloat16 [16384, 7168], P('head', 'ctx'), may hold values from -0.0625 to 0.0625
Outputs:
- attended: bfloat16 [2, 7168], P(None, ('ctx', 'head'))
All inputs are finite; a program needn't handle non-finite values.
Results may differ from a plain program's by a relative error of at most 0.028.
Values may be sent and summed in bfloat16 or wider, within the bound.
No kernel may reach another device: no remote copies, remote signals or barrier semaphores. Data moves between devices by JAX's collectives and lax.ppermute only.
A program may use at most 192 MiB of HBM per device.

v0:
```python
import jax
import jax.numpy as jnp
from jax import lax
from jax.sharding import Mesh
from jax.sharding import PartitionSpec as P

KV_RANK = 512
CTX = ("ctx_0", "ctx_1")
HEAD = ("head_0", "head_1")
CTX_HEAD = ("ctx_0", "ctx_1", "head_0", "head_1")
softmax_scale = 0.07216878


def sent_to_all(x, axis):
    copies = jnp.broadcast_to(x, (lax.axis_size(axis), *x.shape))
    return lax.all_to_all(copies, axis, split_axis=0, concat_axis=0, tiled=True)


def over_copies(x, axis):
    return sent_to_all(x, axis).sum(axis=0)


def in_order(parts, dim):
    parts = jnp.moveaxis(parts, 0, dim)
    lengths = parts.shape
    return parts.reshape(*lengths[:dim], lengths[dim] * lengths[dim + 1], *lengths[dim + 2 :])


def gathered_copies(x, axis, dim):
    return in_order(sent_to_all(x, axis), dim)


def over_copies_2(x, axis):
    return sent_to_all(x, axis).max(axis=0)


def over_axes(x, axes):
    far, near = axes
    nearer = over_copies_2(x, near)
    return over_copies_2(nearer, far)


def in_blocks(x, dim, count):
    before, after = (x.shape[:dim], x.shape[dim + 1 :])
    return jnp.moveaxis(x.reshape(*before, count, -1, *after), dim, 0)


def summed_on_arrival(x, axis, dim):
    count = lax.axis_size(axis)
    parts = lax.all_to_all(in_blocks(x, dim, count), axis, 0, 0, tiled=True)
    return jnp.sum(parts, axis=0)


def sum_in_two_steps(x, axes, dim):
    far, near = axes
    own = summed_on_arrival(in_blocks(x, dim, lax.axis_size(far)), near, dim + 1)
    return jnp.sum(lax.all_to_all(own, far, 0, 0, tiled=True), axis=0)


def side_by_side(arrays, axis, dim, along):
    columns = [a.reshape(*a.shape[:along], -1) for a in arrays]
    both = jnp.concatenate(columns, axis=along)
    filled, at, gathered = (sum_in_two_steps(both, axis, dim), 0, [])
    for a, column in zip(arrays, columns):
        share = filled[..., at : at + column.shape[along]]
        gathered.append(share.reshape(*share.shape[:along], *a.shape[along:]))
        at += column.shape[along]
    return tuple(gathered)


def turned_gather(arrays, axis, dims):
    turned = [jnp.moveaxis(a, dim, 0) for a, dim in zip(arrays, dims)]
    both = jnp.concatenate([t.reshape(len(t), -1) for t in turned], axis=1)
    filled, at, gathered = (lax.all_gather(both, axis, axis=0, tiled=True), 0, [])
    for t, dim in zip(turned, dims):
        share = filled[:, at : at + t[0].size].reshape(-1, *t.shape[1:])
        gathered.append(jnp.moveaxis(share, 0, dim))
        at += t[0].size
    return tuple(gathered)


def on_device(query_low, query_weight, latent_cache, lengths, value_weight, output_weight):
    ctx_count = lax.axis_size(CTX)
    head_count = lax.axis_size(HEAD)
    sequences = query_low.shape[0]
    local_heads = value_weight.shape[0]
    all_heads = local_heads * head_count
    per_share = local_heads // ctx_count
    width = latent_cache.shape[2]
    partial_value = jnp.dot(query_low, query_weight, preferred_element_type=jnp.float32)
    summed = over_copies(partial_value, CTX).astype(jnp.bfloat16)
    gathered = gathered_copies(summed, HEAD, 1)
    queries = gathered.reshape(sequences, all_heads, width)
    span = latent_cache.shape[1]
    offset = (lax.axis_index(CTX) * head_count + lax.axis_index(HEAD)) * span
    places = offset + jnp.arange(span, dtype=jnp.int32)
    usable = (places[None, :] < lengths[:, None])[:, None, :]
    scores = (
        jnp.einsum("bhc,bpc->bhp", queries, latent_cache, preferred_element_type=jnp.float32)
        * softmax_scale
    )
    scores = jnp.where(usable, scores, -1e30)
    local_max = jnp.max(scores, axis=2)
    probabilities = jnp.where(usable, jnp.exp(scores - local_max[..., None]), 0.0)
    totals = jnp.sum(probabilities, axis=2)
    numerators = jnp.einsum(
        "bhp,bpc->bhc",
        probabilities.astype(jnp.bfloat16),
        latent_cache[:, :, :KV_RANK],
        preferred_element_type=jnp.float32,
    )
    highest = over_axes(local_max, (("ctx_0", "ctx_1", "head_0"), "head_1"))
    factor = jnp.exp(local_max - highest)

    def regroup(values):
        dims_now = values.shape
        grouped = values.reshape((sequences, head_count, ctx_count, per_share) + dims_now[2:])
        return jnp.swapaxes(grouped, 1, 2).reshape(dims_now)

    share_totals, share_numerators = side_by_side(
        (regroup(totals * factor), regroup(numerators * factor[..., None])),
        (("ctx_0", "ctx_1", "head_0"), "head_1"),
        1,
        2,
    )
    head_totals, head_numerators = turned_gather((share_totals, share_numerators), CTX, (1, 1))
    latent_out = (head_numerators / head_totals[..., None]).astype(jnp.bfloat16)
    values = jnp.einsum(
        "bhc,hcv->bhv", latent_out, value_weight, preferred_element_type=jnp.float32
    ).astype(jnp.bfloat16)
    projected = jnp.dot(
        values.reshape(sequences, -1), output_weight, preferred_element_type=jnp.float32
    )
    return summed_on_arrival(projected, HEAD, 1).astype(jnp.bfloat16)


def solution(mesh):
    finer = Mesh(mesh.devices.reshape(4, 4, 4, 2), ("ctx_0", "ctx_1", "head_0", "head_1"))
    return jax.shard_map(
        on_device,
        mesh=finer,
        in_specs=(
            P(None, CTX),
            P(CTX, HEAD),
            P(None, CTX_HEAD, None),
            P(),
            P(HEAD, None, None),
            P(HEAD, CTX),
        ),
        out_specs=P(None, CTX_HEAD),
        check_vma=False,
    )
```

profile of v0, /device:TPU:1, one launch (start us, length us, event | category | flops | bytes accessed | tf_op | source)
XLA Modules:
  0.0 125.0 jit_solution(3201359506912485582)
XLA Ops:
  0.0 0.0 copy-start
  0.0 2.0 %fusion.23 = f32[2,9216]{1,0:T(2,128)S(1)} fusion(bf16[2,96]{1,0:T(2,128)(2,1)} %param.6, bf16[96,9216]{1,0:T(8,128)(2,1)} %param.7), kind=kOutput, calls=%fused_computation.30 | convolution fusion | flops 3538944 | bytes 1843584 | tf_op jit(solution)/shard_map/dot_general | solution.py:90
  2.0 1.3 %broadcast_in_dim.37 = f32[16,2,9216]{2,1,0:T(2,128)} broadcast(f32[2,9216]{1,0:T(2,128)S(1)} %fusion.23), dimensions={1,2} | broadcast | bytes 1253376 | tf_op jit(solution)/shard_map/broadcast_in_dim | solution.py:15
  3.3 0.0 copy-start.1
  3.3 7.7 %all-to-all-start = ((f32[16,2,9216]{2,1,0:T(2,128)}), f32[16,2,9216]{2,1,0:T(2,128)S(1)}, u32[]{:S(2)}, u32[]{:S(2)}) async-start(f32[16,2,9216]{2,1,0:T(2,128)} %broadcast_in_dim.37), calls=%async_computation | async-start | bytes 2359296 | tf_op jit(solution)/shard_map/all_to_all | solution.py:16
  11.0 17.0 %all-to-all-done = f32[16,2,9216]{2,1,0:T(2,128)S(1)} async-done(((f32[16,2,9216]{2,1,0:T(2,128)}), f32[16,2,9216]{2,1,0:T(2,128)S(1)}, u32[]{:S(2)}, u32[]{:S(2)}) %all-to-all-start) | async-done | bytes 1179680 | tf_op jit(solution)/shard_map/all_to_all | solution.py:16
  28.0 0.4 reduce_sum.49
  28.4 0.9 broadcast_in_dim.38
  29.3 8.6 %all-to-all-start.1 = ((bf16[8,2,9216]{2,1,0:T(2,128)(2,1)}), bf16[8,2,9216]{2,1,0:T(2,128)(2,1)S(1)}, u32[]{:S(2)}, u32[]{:S(2)}) async-start(bf16[8,2,9216]{2,1,0:T(2,128)(2,1)} %broadcast_in_dim.38), calls=%async_computation.1 | async-start | bytes 589824 | tf_op jit(solution)/shard_map/all_to_all | solution.py:16
  37.9 0.0 copy-done.1
  37.9 0.1 broadcast_compare_fusion
  37.9 6.7 %all-to-all-done.1 = bf16[8,2,9216]{2,1,0:T(2,128)(2,1)S(1)} async-done(((bf16[8,2,9216]{2,1,0:T(2,128)(2,1)}), bf16[8,2,9216]{2,1,0:T(2,128)(2,1)S(1)}, u32[]{:S(2)}, u32[]{:S(2)}) %all-to-all-start.1) | async-done | bytes 294944 | tf_op jit(solution)/shard_map/all_to_all | solution.py:16
  44.6 0.1 copy.32
  44.7 0.3 reshape_reshape.4
  45.0 2.4 %fusion.22 = (f32[2,128]{1,0:T(2,128)S(1)}, f32[2,128,1024]{2,1,0:T(8,128)S(1)}) fusion(bf16[2,128,576]{2,1,0:T(8,128)(2,1)S(1)} %reshape_reshape.4, bf16[2,1024,576]{1,2,0:T(8,128)(2,1)} %param.8, pred[2,1024]{1,0:T(4,128)(4,1)S(1)} %broadcast_compare_fusion), kind=kOutput, calls=%fused_computation.29 | convolution fusion | flops 302776064 | bytes 3705856 | tf_op jit(solution)/shard_map/bhc,bpc->bhp/dot_general | solution.py:99
  47.4 4.4 %all_to_all.35 = f32[2,2,128]{2,1,0:T(2,128)S(1)} all-to-all(f32[2,2,128]{2,1,0:T(2,128)S(1)} %broadcast_in_dim.41), channel_id=1, replica_groups=mesh['ctx_0'=4,'ctx_1'=4,'head_0'=4,'head_1'=2] {'head_1'}, dimensions={0} | all-to-all | bytes 4096 | tf_op jit(solution)/shard_map/all_to_all | solution.py:16
  51.8 0.6 broadcast_in_dim.42
  52.5 4.6 %all-to-all-start.3 = ((f32[64,2,128]{2,1,0:T(2,128)}), f32[64,2,128]{2,1,0:T(2,128)S(1)}, u32[]{:S(2)}, u32[]{:S(2)}) async-start(f32[64,2,128]{2,1,0:T(2,128)} %broadcast_in_dim.42), calls=%async_computation.3 | async-start | bytes 131072 | tf_op jit(solution)/shard_map/all_to_all | solution.py:16
  57.1 0.3 fusion.10
  57.4 8.1 %all-to-all-done.3 = f32[64,2,128]{2,1,0:T(2,128)S(1)} async-done(((f32[64,2,128]{2,1,0:T(2,128)}), f32[64,2,128]{2,1,0:T(2,128)S(1)}, u32[]{:S(2)}, u32[]{:S(2)}) %all-to-all-start.3) | async-done | bytes 65568 | tf_op jit(solution)/shard_map/all_to_all | solution.py:16
  65.5 0.1 reduce_max.29
  65.6 2.4 %fusion.3 = f32[2,128,512]{2,1,0:T(8,128)S(1)} fusion(bf16[2,1024,576]{1,2,0:T(8,128)(2,1)} %param.8, f32[2,128,1024]{2,1,0:T(8,128)S(1)} %get-tuple-element.8, f32[2,128]{1,0:T(2,128)S(1)} %get-tuple-element.7, pred[2,1024]{1,0:T(4,128)(4,1)S(1)} %broadcast_compare_fusion, f32[2,128]{1,0:T(2,128)S(1)} %get-tuple-element.6), kind=kOutput, calls=%fused_computation.4 | convolution fusion | flops 269352960 | bytes 3674112 | tf_op jit(solution)/shard_map/bhp,bpc->bhc/dot_general | solution.py:106
  68.1 0.4 copy.37
  68.5 0.1 mul.46
  68.6 0.1 copy.41
  68.7 0.1 reshape.98
  68.8 0.7 maximum_bitcast_fusion
  69.6 0.1 copy.39
  69.7 5.6 %all_to_all.36 = f32[2,64,2,1,513]{4,2,1,3,0:T(2,128)S(1)} all-to-all(f32[2,64,2,1,513]{4,2,1,3,0:T(2,128)S(1)} %copy.39), channel_id=1, replica_groups=mesh['ctx_0'=4,'ctx_1'=4,'head_0'=4,'head_1'=2] {'head_1'}, dimensions={0} | all-to-all | bytes 1050624 | tf_op jit(solution)/shard_map/all_to_all | solution.py:50
  75.3 0.6 reduce_sum.51
  75.9 14.7 %all_to_all.37 = f32[64,2,1,513]{3,1,2,0:T(2,128)S(1)} all-to-all(f32[64,2,1,513]{3,1,2,0:T(2,128)S(1)} %bitcast.59), channel_id=1, replica_groups=mesh['ctx_0'=4,'ctx_1'=4,'head_0'=4,'head_1'=2] {'ctx_0','ctx_1','head_0'}, dimensions={0} | all-to-all | bytes 525312 | tf_op jit(solution)/shard_map/all_to_all | solution.py:57
  90.6 0.1 reduce_sum.53
  90.8 0.1 slice_bitcast_fusion.1
  90.8 0.1 slice_reduce_fusion
  91.0 0.1 maximum_bitcast_fusion.1
  91.0 16.2 %all-gather = f32[16,1,1026]{2,1,0:T(1,128)S(1)} all-gather(f32[1,1,1026]{2,1,0:T(1,128)S(1)} %maximum_bitcast_fusion.1), channel_id=1, replica_groups=mesh['ctx_0'=4,'ctx_1'=4,'head_0'=4,'head_1'=2] {'ctx_0','ctx_1'}, dimensions={0}, use_global_device_ids=true | all-gather | bytes 69768 | tf_op jit(solution)/shard_map/all_gather | solution.py:74
  107.3 0.1 slice.22
  107.4 0.1 reshape.93
  107.4 0.0 copy-done
  107.4 2.7 %fusion.8 = f32[8,2,56]{2,1,0:T(2,128)S(1)} fusion(bf16[8,56,2048]{2,1,0:T(8,128)(2,1)} %bitcast.58, bf16[16,512,128]{2,1,0:T(8,128)(2,1)S(1)} %copy-done, f32[16,2,512]{2,1,0:T(2,128)S(1)} %reshape.93, f32[2,16]{0,1:T(8,128)S(1)} %slice_bitcast_fusion), kind=kOutput, calls=%fused_computation.8 | convolution fusion | flops 7901184 | bytes 4001408 | tf_op jit(solution)/shard_map/dot_general | solution.py:131
  110.1 14.3 %all_to_all.38 = f32[8,2,56]{2,1,0:T(2,128)S(1)} all-to-all(f32[8,2,56]{2,1,0:T(2,128)S(1)} %fusion.8), channel_id=1, replica_groups=mesh['ctx_0'=4,'ctx_1'=4,'head_0'=4,'head_1'=2] {'head_0','head_1'}, dimensions={0} | all-to-all | bytes 7168 | tf_op jit(solution)/shard_map/all_to_all | solution.py:50
  124.5 0.5 reduce_sum.55
  (7 shorter events, 0.0 us)
Async XLA Ops:
  0.0 107.4 %copy-start = (bf16[16,512,128]{2,1,0:T(8,128)(2,1)S(1)}, bf16[16,512,128]{2,1,0:T(8,128)(2,1)}, u32[]{:S(2)}) copy-start(bf16[16,512,128]{2,1,0:T(8,128)(2,1)} %param.10) | copy-start | bytes 6291460
  3.3 34.6 %copy-start.1 = (s32[2]{0:T(128)S(1)}, s32[2]{0:T(128)}, u32[]{:S(2)}) copy-start(s32[2]{0:T(128)} %param.9) | copy-start | bytes 28
  3.3 24.7 %all-to-all-start = ((f32[16,2,9216]{2,1,0:T(2,128)}), f32[16,2,9216]{2,1,0:T(2,128)S(1)}, u32[]{:S(2)}, u32[]{:S(2)}) async-start(f32[16,2,9216]{2,1,0:T(2,128)} %broadcast_in_dim.37), calls=%async_computation | async-start | bytes 2359296 | tf_op jit(solution)/shard_map/all_to_all | solution.py:16
  29.3 15.3 %all-to-all-start.1 = ((bf16[8,2,9216]{2,1,0:T(2,128)(2,1)}), bf16[8,2,9216]{2,1,0:T(2,128)(2,1)S(1)}, u32[]{:S(2)}, u32[]{:S(2)}) async-start(bf16[8,2,9216]{2,1,0:T(2,128)(2,1)} %broadcast_in_dim.38), calls=%async_computation.1 | async-start | bytes 589824 | tf_op jit(solution)/shard_map/all_to_all | solution.py:16
  52.5 13.1 %all-to-all-start.3 = ((f32[64,2,128]{2,1,0:T(2,128)}), f32[64,2,128]{2,1,0:T(2,128)S(1)}, u32[]{:S(2)}, u32[]{:S(2)}) async-start(f32[64,2,128]{2,1,0:T(2,128)} %broadcast_in_dim.42), calls=%async_computation.3 | async-start | bytes 131072 | tf_op jit(solution)/shard_map/all_to_all | solution.py:16
where the time goes:
time: 126 us; the launch traced here: 125 us
  blocking collectives  55.4 us (44%)
  waiting for transfers between devices  31.8 us (25%)
  starting transfers between devices  20.9 us (17%)
  matrix products  9.5 us (8%)
  local copies, waits for them, and re-layouts  4.34 us (3%)
  other arithmetic  2.99 us (2%)
    all_to_all x3, waiting for transfers between devices, sent_to_all(): return lax.all_to_all(copies, axis, split_axis=0, concat_axis=0, tiled=True)  31.8 us
    all_to_all x3, starting transfers between devices, sent_to_all(): return lax.all_to_all(copies, axis, split_axis=0, concat_axis=0, tiled=True)  20.9 us
    all_to_all x2, blocking collectives, summed_on_arrival(): parts = lax.all_to_all(in_blocks(x, dim, count), axis, 0, 0, tiled=True)  20 us
    all_gather x1, blocking collectives, turned_gather(): lax.all_gather(both, axis, axis=0, tiled=True)  16.2 us
    all_to_all x1, blocking collectives, sum_in_two_steps(): return jnp.sum(lax.all_to_all(own, far, 0, 0, tiled=True), axis=0)  14.7 us
    all_to_all x1, blocking collectives, sent_to_all(): return lax.all_to_all(copies, axis, split_axis=0, concat_axis=0, tiled=True)  4.44 us
    broadcast_in_dim x4, local copies, waits for them, and re-layouts, sent_to_all(): copies = jnp.broadcast_to(x, (lax.axis_size(axis), *x.shape))  2.82 us
    dot_general x1, matrix products, on_device(): jnp.dot(values.reshape(sequences, -1), output_weight, preferred_element_t...  2.71 us
  transfers between devices with their start and end apart: 3, of which 3 were waited for; matrix products, arithmetic and copies ran while one was open for 0% of the time, Pallas kernels for 0%

commit v1 on v0

--- a/solution.py
+++ b/solution.py
@@ -71,7 +71,13 @@
 def turned_gather(arrays, axis, dims):
     turned = [jnp.moveaxis(a, dim, 0) for a, dim in zip(arrays, dims)]
     both = jnp.concatenate([t.reshape(len(t), -1) for t in turned], axis=1)
-    filled, at, gathered = (lax.all_gather(both, axis, axis=0, tiled=True), 0, [])
+    filled, at, gathered = (
+        jnp.concatenate(
+            lax.all_to_all(jnp.stack([both] * lax.axis_size(axis)), axis, 0, 0), axis=0
+        ),
+        0,
+        [],
+    )
     for t, dim in zip(turned, dims):
         share = filled[:, at : at + t[0].size].reshape(-1, *t.shape[1:])
         gathered.append(jnp.moveaxis(share, 0, dim))

time: 126 us -> 115 us (0.913)
  blocking collectives: 55.4 us -> 44.4 us
    all_gather x1 -> x0, blocking collectives: 16.2 us -> none  [turned_gather(): lax.all_gather(both, axis, axis=0, tiled=True)]
    all_to_all x0 -> x1, blocking collectives: none -> 9.29 us  [turned_gather(): lax.all_to_all(jnp.stack([both] * lax.axis_size(axis)), axis, 0, 0)]
    all_to_all x2, blocking collectives: 20 us -> 15.9 us  [summed_on_arrival(): parts = lax.all_to_all(in_blocks(x, dim, count), axis, 0, 0, tiled=True)]
where the time goes in v1:
time: 115 us; the launch traced here: 114 us
  blocking collectives  44.4 us (39%)
  waiting for transfers between devices  31.8 us (28%)
  starting transfers between devices  20.9 us (18%)
  matrix products  9.5 us (8%)
  local copies, waits for them, and re-layouts  4.38 us (4%)
  other arithmetic  3 us (3%)
    all_to_all x3, waiting for transfers between devices, sent_to_all(): return lax.all_to_all(copies, axis, split_axis=0, concat_axis=0, tiled=True)  31.8 us
    all_to_all x3, starting transfers between devices, sent_to_all(): return lax.all_to_all(copies, axis, split_axis=0, concat_axis=0, tiled=True)  20.9 us
    all_to_all x2, blocking collectives, summed_on_arrival(): parts = lax.all_to_all(in_blocks(x, dim, count), axis, 0, 0, tiled=True)  15.9 us
    all_to_all x1, blocking collectives, sum_in_two_steps(): return jnp.sum(lax.all_to_all(own, far, 0, 0, tiled=True), axis=0)  14.7 us
    all_to_all x1, blocking collectives, turned_gather(): lax.all_to_all(jnp.stack([both] * lax.axis_size(axis)), axis, 0, 0)  9.29 us
    all_to_all x1, blocking collectives, sent_to_all(): return lax.all_to_all(copies, axis, split_axis=0, concat_axis=0, tiled=True)  4.44 us
    broadcast_in_dim x4, local copies, waits for them, and re-layouts, sent_to_all(): copies = jnp.broadcast_to(x, (lax.axis_size(axis), *x.shape))  2.82 us
    dot_general x1, matrix products, on_device(): jnp.dot(values.reshape(sequences, -1), output_weight, preferred_element_t...  2.71 us
  transfers between devices with their start and end apart: 3, of which 3 were waited for; matrix products, arithmetic and copies ran while one was open for 0% of the time, Pallas kernels for 0%

profile of v1, /device:TPU:1, one launch (start us, length us, event | category | flops | bytes accessed | tf_op | source)
XLA Modules:
  0.0 114.1 jit_solution(16575330218785610403)
XLA Ops:
  0.0 0.0 copy-start
  0.0 2.0 %fusion.23 = f32[2,9216]{1,0:T(2,128)S(1)} fusion(bf16[2,96]{1,0:T(2,128)(2,1)} %param.6, bf16[96,9216]{1,0:T(8,128)(2,1)} %param.7), kind=kOutput, calls=%fused_computation.30 | convolution fusion | flops 3538944 | bytes 1843584 | tf_op jit(solution)/shard_map/dot_general | solution.py:96
  2.0 1.3 %broadcast_in_dim.37 = f32[16,2,9216]{2,1,0:T(2,128)} broadcast(f32[2,9216]{1,0:T(2,128)S(1)} %fusion.23), dimensions={1,2} | broadcast | bytes 1253376 | tf_op jit(solution)/shard_map/broadcast_in_dim | solution.py:15
  3.3 0.0 copy-start.1
  3.3 7.7 %all-to-all-start = ((f32[16,2,9216]{2,1,0:T(2,128)}), f32[16,2,9216]{2,1,0:T(2,128)S(1)}, u32[]{:S(2)}, u32[]{:S(2)}) async-start(f32[16,2,9216]{2,1,0:T(2,128)} %broadcast_in_dim.37), calls=%async_computation | async-start | bytes 2359296 | tf_op jit(solution)/shard_map/all_to_all | solution.py:16
  11.0 17.0 %all-to-all-done = f32[16,2,9216]{2,1,0:T(2,128)S(1)} async-done(((f32[16,2,9216]{2,1,0:T(2,128)}), f32[16,2,9216]{2,1,0:T(2,128)S(1)}, u32[]{:S(2)}, u32[]{:S(2)}) %all-to-all-start) | async-done | bytes 1179680 | tf_op jit(solution)/shard_map/all_to_all | solution.py:16
  28.0 0.4 reduce_sum.49
  28.4 0.9 broadcast_in_dim.38
  29.3 8.6 %all-to-all-start.1 = ((bf16[8,2,9216]{2,1,0:T(2,128)(2,1)}), bf16[8,2,9216]{2,1,0:T(2,128)(2,1)S(1)}, u32[]{:S(2)}, u32[]{:S(2)}) async-start(bf16[8,2,9216]{2,1,0:T(2,128)(2,1)} %broadcast_in_dim.38), calls=%async_computation.1 | async-start | bytes 589824 | tf_op jit(solution)/shard_map/all_to_all | solution.py:16
  37.9 0.0 copy-done.1
  37.9 0.1 broadcast_compare_fusion
  37.9 6.7 %all-to-all-done.1 = bf16[8,2,9216]{2,1,0:T(2,128)(2,1)S(1)} async-done(((bf16[8,2,9216]{2,1,0:T(2,128)(2,1)}), bf16[8,2,9216]{2,1,0:T(2,128)(2,1)S(1)}, u32[]{:S(2)}, u32[]{:S(2)}) %all-to-all-start.1) | async-done | bytes 294944 | tf_op jit(solution)/shard_map/all_to_all | solution.py:16
  44.6 0.1 copy.32
  44.7 0.3 reshape_reshape.4
  45.0 2.4 %fusion.22 = (f32[2,128]{1,0:T(2,128)S(1)}, f32[2,128,1024]{2,1,0:T(8,128)S(1)}) fusion(bf16[2,128,576]{2,1,0:T(8,128)(2,1)S(1)} %reshape_reshape.4, bf16[2,1024,576]{1,2,0:T(8,128)(2,1)} %param.8, pred[2,1024]{1,0:T(4,128)(4,1)S(1)} %broadcast_compare_fusion), kind=kOutput, calls=%fused_computation.29 | convolution fusion | flops 302776064 | bytes 3705856 | tf_op jit(solution)/shard_map/bhc,bpc->bhp/dot_general | solution.py:105
  47.4 4.4 %all_to_all.40 = f32[2,2,128]{2,1,0:T(2,128)S(1)} all-to-all(f32[2,2,128]{2,1,0:T(2,128)S(1)} %broadcast_in_dim.41), channel_id=1, replica_groups=mesh['ctx_0'=4,'ctx_1'=4,'head_0'=4,'head_1'=2] {'head_1'}, dimensions={0} | all-to-all | bytes 4096 | tf_op jit(solution)/shard_map/all_to_all | solution.py:16
  51.8 0.6 broadcast_in_dim.42
  52.5 4.6 %all-to-all-start.3 = ((f32[64,2,128]{2,1,0:T(2,128)}), f32[64,2,128]{2,1,0:T(2,128)S(1)}, u32[]{:S(2)}, u32[]{:S(2)}) async-start(f32[64,2,128]{2,1,0:T(2,128)} %broadcast_in_dim.42), calls=%async_computation.3 | async-start | bytes 131072 | tf_op jit(solution)/shard_map/all_to_all | solution.py:16
  57.1 0.3 fusion.10
  57.4 8.1 %all-to-all-done.3 = f32[64,2,128]{2,1,0:T(2,128)S(1)} async-done(((f32[64,2,128]{2,1,0:T(2,128)}), f32[64,2,128]{2,1,0:T(2,128)S(1)}, u32[]{:S(2)}, u32[]{:S(2)}) %all-to-all-start.3) | async-done | bytes 65568 | tf_op jit(solution)/shard_map/all_to_all | solution.py:16
  65.5 0.1 reduce_max.29
  65.6 2.4 %fusion.3 = f32[2,128,512]{2,1,0:T(8,128)S(1)} fusion(bf16[2,1024,576]{1,2,0:T(8,128)(2,1)} %param.8, f32[2,128,1024]{2,1,0:T(8,128)S(1)} %get-tuple-element.8, f32[2,128]{1,0:T(2,128)S(1)} %get-tuple-element.7, pred[2,1024]{1,0:T(4,128)(4,1)S(1)} %broadcast_compare_fusion, f32[2,128]{1,0:T(2,128)S(1)} %get-tuple-element.6), kind=kOutput, calls=%fused_computation.4 | convolution fusion | flops 269352960 | bytes 3674112 | tf_op jit(solution)/shard_map/bhp,bpc->bhc/dot_general | solution.py:112
  68.1 0.4 copy.37
  68.5 0.1 mul.46
  68.6 0.1 copy.41
  68.7 0.1 reshape.103
  68.8 0.7 maximum_bitcast_fusion
  69.6 0.1 copy.39
  69.7 5.6 %all_to_all.41 = f32[2,64,2,1,513]{4,2,1,3,0:T(2,128)S(1)} all-to-all(f32[2,64,2,1,513]{4,2,1,3,0:T(2,128)S(1)} %copy.39), channel_id=1, replica_groups=mesh['ctx_0'=4,'ctx_1'=4,'head_0'=4,'head_1'=2] {'head_1'}, dimensions={0} | all-to-all | bytes 1050624 | tf_op jit(solution)/shard_map/all_to_all | solution.py:50
  75.3 0.6 reduce_sum.51
  75.9 14.7 %all_to_all.42 = f32[64,2,1,513]{3,1,2,0:T(2,128)S(1)} all-to-all(f32[64,2,1,513]{3,1,2,0:T(2,128)S(1)} %bitcast.57), channel_id=1, replica_groups=mesh['ctx_0'=4,'ctx_1'=4,'head_0'=4,'head_1'=2] {'ctx_0','ctx_1','head_0'}, dimensions={0} | all-to-all | bytes 525312 | tf_op jit(solution)/shard_map/all_to_all | solution.py:57
  90.6 0.1 reduce_sum.53
  90.8 0.1 slice_bitcast_fusion.1
  90.8 0.1 slice_reduce_fusion
  91.0 0.1 maximum_reduce_fusion
  91.1 9.3 %all_to_all.43 = f32[16,1,1026]{2,1,0:T(1,128)S(1)} all-to-all(f32[16,1,1026]{2,1,0:T(1,128)S(1)} %stack.2), channel_id=1, replica_groups=mesh['ctx_0'=4,'ctx_1'=4,'head_0'=4,'head_1'=2] {'ctx_0','ctx_1'}, dimensions={0} | all-to-all | bytes 131328 | tf_op jit(solution)/shard_map/all_to_all | solution.py:76
  100.4 0.1 slice.22
  100.5 0.1 reshape.100
  100.6 0.0 copy-done
  100.6 2.7 %fusion.8 = f32[8,2,56]{2,1,0:T(2,128)S(1)} fusion(bf16[8,56,2048]{2,1,0:T(8,128)(2,1)} %bitcast.56, bf16[16,512,128]{2,1,0:T(8,128)(2,1)S(1)} %copy-done, f32[16,2,512]{2,1,0:T(2,128)S(1)} %reshape.100, f32[2,16]{0,1:T(8,128)S(1)} %slice_bitcast_fusion), kind=kOutput, calls=%fused_computation.8 | convolution fusion | flops 7901184 | bytes 4001408 | tf_op jit(solution)/shard_map/dot_general | solution.py:137
  103.3 10.3 %all_to_all.44 = f32[8,2,56]{2,1,0:T(2,128)S(1)} all-to-all(f32[8,2,56]{2,1,0:T(2,128)S(1)} %fusion.8), channel_id=1, replica_groups=mesh['ctx_0'=4,'ctx_1'=4,'head_0'=4,'head_1'=2] {'head_0','head_1'}, dimensions={0} | all-to-all | bytes 7168 | tf_op jit(solution)/shard_map/all_to_all | solution.py:50
  113.6 0.5 reduce_sum.55
  (8 shorter events, 0.1 us)
Async XLA Ops:
  0.0 100.6 %copy-start = (bf16[16,512,128]{2,1,0:T(8,128)(2,1)S(1)}, bf16[16,512,128]{2,1,0:T(8,128)(2,1)}, u32[]{:S(2)}) copy-start(bf16[16,512,128]{2,1,0:T(8,128)(2,1)} %param.10) | copy-start | bytes 6291460
  3.3 34.6 %copy-start.1 = (s32[2]{0:T(128)S(1)}, s32[2]{0:T(128)}, u32[]{:S(2)}) copy-start(s32[2]{0:T(128)} %param.9) | copy-start | bytes 28
  3.3 24.7 %all-to-all-start = ((f32[16,2,9216]{2,1,0:T(2,128)}), f32[16,2,9216]{2,1,0:T(2,128)S(1)}, u32[]{:S(2)}, u32[]{:S(2)}) async-start(f32[16,2,9216]{2,1,0:T(2,128)} %broadcast_in_dim.37), calls=%async_computation | async-start | bytes 2359296 | tf_op jit(solution)/shard_map/all_to_all | solution.py:16
  29.3 15.3 %all-to-all-start.1 = ((bf16[8,2,9216]{2,1,0:T(2,128)(2,1)}), bf16[8,2,9216]{2,1,0:T(2,128)(2,1)S(1)}, u32[]{:S(2)}, u32[]{:S(2)}) async-start(bf16[8,2,9216]{2,1,0:T(2,128)(2,1)} %broadcast_in_dim.38), calls=%async_computation.1 | async-start | bytes 589824 | tf_op jit(solution)/shard_map/all_to_all | solution.py:16
  52.5 13.1 %all-to-all-start.3 = ((f32[64,2,128]{2,1,0:T(2,128)}), f32[64,2,128]{2,1,0:T(2,128)S(1)}, u32[]{:S(2)}, u32[]{:S(2)}) async-start(f32[64,2,128]{2,1,0:T(2,128)} %broadcast_in_dim.42), calls=%async_computation.3 | async-start | bytes 131072 | tf_op jit(solution)/shard_map/all_to_all | solution.py:16
